TPU v7x, 32 devices: a 4x4x1 block of a 4x4x8 slice. The times are simulated.
32 devices in a mesh: rep: 1 (over z), dp: 32 (over x, y, core).
Axes of the slice: x: 4, y: 4, z: 1, core: 2. Of those that a mesh axis runs over, the one named last changes fastest.
The devices are a block of a 4x4x8 slice.
Arguments:
- a: bfloat16 [32, 2, 4096, 512], P(('rep', 'dp'))
- g: bfloat16 [32, 2, 4096, 4096], P(('rep', 'dp'))
Outputs:
- output: bfloat16 [2, 512, 4096], P('rep')
All inputs are finite; a program needn't handle non-finite values.
Results may differ from a plain program's by a relative error of at most 0.012.
Values are sent between devices in bfloat16 or wider.
A program may use at most 768 MiB of HBM per device.

v0:
```python
import jax
import jax.numpy as jnp


def solution(mesh):
    groups = mesh.shape["rep"]

    def step(a, g):
        a, g = (t.reshape(groups, -1, *t.shape[1:]) for t in (a, g))
        sums = jnp.einsum("rsntd,rsntf->rndf", a, g, preferred_element_type=jnp.float32)
        return sums.astype(jnp.bfloat16).reshape(-1, *sums.shape[2:])

    return step
```

profile of v0, /device:TPU:97, one launch (start us, length us, event | category | flops | bytes accessed | tf_op | source)
XLA Modules:
  0.0 178.3 jit_solution(18306532789618784375)
XLA Ops:
  0.0 45.1 %fusion = f32[2,512,4096]{2,1,0:T(8,128)} fusion(bf16[1,2,4096,4096]{3,2,1,0:T(8,128)(2,1)} %param.1, bf16[1,2,4096,512]{3,2,1,0:T(8,128)(2,1)} %param), kind=kOutput, calls=%fused_computation | convolution fusion | flops 34359738368 | bytes 92274688 | tf_op jit(solution)/rsntd,rsntf->rndf/dot_general | solution.py:10
  45.1 133.3 %all-reduce.2 = bf16[2,512,4096]{2,1,0:T(8,128)(2,1)} all-reduce(f32[2,512,4096]{2,1,0:T(8,128)} %fusion), channel_id=1, replica_groups=mesh['axis_0'=32] {'axis_0'}, use_global_device_ids=true, to_apply=%add.clone | all-reduce | flops 4194304 | bytes 25165824 | tf_op jit(solution)/rsntd,rsntf->rndf/dot_general | solution.py:10
where the time goes:
time: 178 us
  blocking collectives  133 us (75%)
  matrix products  45.1 us (25%)
    dot_general x1, blocking collectives, step(): jnp.einsum('rsntd,rsntf->rndf', a, g, preferred_element_type=jnp.float32)  133 us
    dot_general x1, matrix products, step(): jnp.einsum('rsntd,rsntf->rndf', a, g, preferred_element_type=jnp.float32)  45.1 us

commit v1 on v0

v1 whole, which is shorter than its diff:
```python
import functools
import math

import jax
import jax.numpy as jnp
from jax import lax
from jax.experimental import pallas as pl
from jax.experimental.pallas import tpu as pltpu
from jax.sharding import PartitionSpec as P

MESH = pl.DeviceIdType.MESH
F32, BF16 = jnp.float32, jnp.bfloat16
LANES = 128
COLS = 4 * LANES


def kernel(side, a_ref, g_ref, out_ref, av, gv, acc, mid, es, er, s1, r1, s2, r2, s3, r3, s4, r4, ag,
           a_sem, g_sem, o_sem, send_sem, e_r, r1_r, r2_r, r3_r, r4_r, g1_r, g2_r, g3_r, g4_r, z_r):
    chunks, rows = es.shape[0], es.shape[1]
    splits = av.shape[1]
    block, piece = rows // side, rows // side // side
    ring = acc.shape[0]

    me = lax.axis_index("dp")
    core = lax.rem(me, 2)
    y = lax.rem(lax.div(me, 2), side)
    x = lax.div(me, 2 * side)

    def device(x, y, core):
        return {"dp": (x * side + y) * 2 + core}

    def up(p, by=1):
        return lax.rem(p + by, side)

    peer = device(x, y, 1 - core)
    along = (
        (device(up(x), y, core), device(up(x, side - 1), y, core)),
        (device(x, up(y), core), device(x, up(y, side - 1), core)),
    )
    place = (x, y)

    def a_copy(m, h):
        matrix = 1 - core if m == 0 else core
        return pltpu.make_async_copy(a_ref.at[0, matrix, :, pl.ds(h * rows, rows)], av.at[m, h], a_sem.at[m, h])

    def g_copy(m, j, slot):
        matrix = 1 - core if m == 0 else core
        columns = pl.ds(pl.multiple_of(j * COLS, COLS), COLS)
        return pltpu.make_async_copy(g_ref.at[0, matrix, :, columns], gv.at[m, slot], g_sem.at[m, slot])

    for m in range(2):
        a_copy(m, 0).start()
        g_copy(m, 0, 0).start()
    for m in range(2):
        for h in range(1, splits):
            a_copy(m, h).start()

    barrier = pltpu.get_barrier_semaphore()
    partners = (peer, *along[0], *along[1])
    for partner in partners:
        pl.semaphore_signal(barrier, inc=1, device_id=partner, device_id_type=MESH)
    pl.semaphore_wait(barrier, len(partners))

    def remote(src, dst, stage, recv, to):
        return pltpu.make_async_remote_copy(
            src_ref=src, dst_ref=dst, send_sem=send_sem.at[stage], recv_sem=recv, device_id=to, device_id_type=MESH)

    def e_copy(s):
        return remote(es.at[s], er.at[s], 0, e_r.at[s], peer)

    def z_copy(s):
        return remote(ag.at[0, s], ag.at[1, s], 1, z_r.at[s], peer)

    def r_copy(stage, src, dst, sem, axis, s, part, way):
        return remote(src.at[s, part, way], dst.at[s, part, way], stage, sem.at[s, part, way], along[axis][way])

    r1_copy = functools.partial(r_copy, 2, s1, r1, r1_r)
    r2_copy = functools.partial(r_copy, 3, s2, r2, r2_r)
    r3_copy = functools.partial(r_copy, 4, s3, r3, r3_r)
    r4_copy = functools.partial(r_copy, 5, s4, r4, r4_r)

    def g_send(stage, view, sem, axis, s, part, way):
        return remote(view, view, stage, sem.at[s, part, way], along[axis][way])

    def two(part):
        return pl.ds(2 * part, 2)

    def at(p, size):
        return pl.ds(pl.multiple_of(p * size, size), size)

    def g1_copy(s, part, way):
        p, q = place[part], place[1 - part]
        return g_send(6, ag.at[0, s, two(part), at(p * side + q, piece)], g1_r, 1 - part, s, part, way)

    def g2_copy(s, part, way):
        p, q = place[part], place[1 - part]
        q = up(q, side - 1) if way == 0 else up(q)
        return g_send(7, ag.at[0, s, 2 * part + way, at(p * side + q, piece)], g2_r, 1 - part, s, part, way)

    def g3_copy(s, part, way):
        return g_send(8, ag.at[0, s, two(part), at(place[part], block)], g3_r, part, s, part, way)

    def g4_copy(s, part, way):
        p = place[part]
        p = up(p, side - 1) if way == 0 else up(p)
        return g_send(9, ag.at[0, s, 2 * part + way, at(p, block)], g4_r, part, s, part, way)

    def out_copies(m, s):
        matrix = core if m == 0 else 1 - core
        j, h = lax.div(s, splits), lax.rem(s, splits)
        for k in range(COLS // LANES):
            yield pltpu.make_async_copy(
                ag.at[m, s, k],
                out_ref.at[matrix, at(h, rows), pl.ds(pl.multiple_of(j * COLS + k * LANES, LANES), LANES)],
                o_sem)

    both = [(part, way) for part in range(2) for way in range(2)]

    def lane(part, half):
        return slice((2 * part + half) * LANES, (2 * part + half + 1) * LANES)

    def start_r1(s):
        c = lax.rem(s, ring)
        for part in range(2):
            p = place[part]

            def take(q, half):
                return acc[c, at(q, block), lane(part, half)].astype(BF16)

            s1[s, part, 0, 0] = take(up(p, 2), 0)
            s1[s, part, 0, 1] = take(up(p), 1)
            s1[s, part, 1, 0] = take(up(p, 2), 1)
            s1[s, part, 1, 1] = take(up(p, side - 1), 0)
            for way in range(2):
                r1_copy(part, s, part, way).start()

    def do_r2(s):
        c = lax.rem(s, ring)
        for part, way in both:
            r1_copy(part, s, part, way).wait_recv()
            p = place[part]
            q = up(p) if way == 0 else up(p, side - 1)
            s2[s, part, way] = (acc[c, at(q, block), lane(part, way)] + r1[s, part, way, 0].astype(F32)).astype(BF16)
            r2_copy(part, s, part, way).start()

    def do_r3(s):
        c = lax.rem(s, ring)
        for part in range(2):
            p, q = place[part], place[1 - part]
            for way in range(2):
                r2_copy(part, s, part, way).wait_recv()
                mid[c, part, way] = (acc[c, at(p, block), lane(part, way)] + r1[s, part, 1 - way, 1].astype(F32)
                                     + r2[s, part, way].astype(F32))

            def take(r, half):
                return mid[c, part, half, at(r, piece)].astype(BF16)

            s3[s, part, 0, 0] = take(up(q, 2), 0)
            s3[s, part, 0, 1] = take(up(q), 1)
            s3[s, part, 1, 0] = take(up(q, 2), 1)
            s3[s, part, 1, 1] = take(up(q, side - 1), 0)
            for way in range(2):
                r3_copy(1 - part, s, part, way).start()

    def do_r4(s):
        c = lax.rem(s, ring)
        for part, way in both:
            r3_copy(1 - part, s, part, way).wait_recv()
            q = place[1 - part]
            r = up(q) if way == 0 else up(q, side - 1)
            s4[s, part, way] = (mid[c, part, way, at(r, piece)] + r3[s, part, way, 0].astype(F32)).astype(BF16)
            r4_copy(1 - part, s, part, way).start()

    def do_g1(s):
        c = lax.rem(s, ring)
        for part in range(2):
            p, q = place[part], place[1 - part]
            for way in range(2):
                r4_copy(1 - part, s, part, way).wait_recv()
                total = (mid[c, part, way, at(q, piece)] + r3[s, part, 1 - way, 1].astype(F32)
                         + r4[s, part, way].astype(F32))
                ag[0, s, 2 * part + way, at(p * side + q, piece)] = total.astype(BF16)
            for way in range(2):
                g1_copy(s, part, way).start()

    def do_g2(s):
        for part, way in both:
            g1_copy(s, part, way).wait_recv()
            g2_copy(s, part, way).start()

    def do_g3(s):
        for part in range(2):
            for way in range(2):
                g2_copy(s, part, way).wait_recv()
            for way in range(2):
                g3_copy(s, part, way).start()

    def do_g4(s):
        for part, way in both:
            g3_copy(s, part, way).wait_recv()
            g4_copy(s, part, way).start()

    def do_z(s):
        for part, way in both:
            g4_copy(s, part, way).wait_recv()
        z_copy(s).start()
        for copy in out_copies(0, s):
            copy.start()

    def do_end(s):
        z_copy(s).wait_recv()
        for copy in out_copies(1, s):
            copy.start()

    later = [do_r2, do_r3, do_r4, do_g1, do_g2, do_g3, do_g4, do_z, do_end]

    def term(m, h, slot):
        return lax.dot_general(av[m, h], gv[m, slot], (((0,), (0,)), ((), ())), preferred_element_type=F32)

    def turn(i, carry):
        j, h = lax.div(i, splits), lax.rem(i, splits)
        slot = lax.rem(j, 2)
        computes = i < chunks

        @pl.when(computes)
        def _():
            @pl.when(h == 0)
            def _():
                @pl.when(i + splits < chunks)
                def _():
                    for m in range(2):
                        g_copy(m, j + 1, 1 - slot).start()

                g_copy(0, j, slot).wait()

            @pl.when(j == 0)
            def _():
                a_copy(0, h).wait()

            es[i] = term(0, h, slot).astype(BF16)
            e_copy(i).start()

        for n in reversed(range(len(later))):
            s = i - (n + 1)

            @pl.when((s >= 0) & (s < chunks))
            def _():
                later[n](s)

        @pl.when(computes)
        def _():
            @pl.when(h == 0)
            def _():
                g_copy(1, j, slot).wait()

            @pl.when(j == 0)
            def _():
                a_copy(1, h).wait()

            c = lax.rem(i, ring)
            acc[c] = term(1, h, slot)
            e_copy(i).wait_recv()
            acc[c] += er[i].astype(F32)
            start_r1(i)

        return carry

    lax.fori_loop(0, chunks + len(later), turn, 0)

    sent = [es, es, s1, s2, s3, s4, s3, s4, s1, s2]
    for stage, ref in enumerate(sent):
        pltpu.make_async_copy(ref, ref, send_sem.at[stage]).wait()
    pltpu.make_async_copy(ag, ag, o_sem).wait()


def solution(mesh):
    side = math.isqrt(mesh.shape["dp"] // 2)

    def step(a, g):
        _, matrices, tokens, d = a.shape
        ff = g.shape[3]
        assert matrices == 2 and side == 4
        splits = 2
        rows = d // splits
        chunks = splits * ff // COLS
        block, piece = rows // side, rows // side // side

        def halves(n, *shape):
            return pltpu.VMEM((chunks, 2, 2, *n, *shape, LANES), BF16)

        dma = pltpu.SemaphoreType.DMA
        return pl.pallas_call(
            functools.partial(kernel, side),
            out_shape=jax.ShapeDtypeStruct((matrices, d, ff), BF16),
            in_specs=[pl.BlockSpec(memory_space=pl.ANY)] * 2,
            out_specs=pl.BlockSpec(memory_space=pl.ANY),
            scratch_shapes=[
                pltpu.VMEM((2, splits, tokens, rows), BF16),
                pltpu.VMEM((2, 2, tokens, COLS), BF16),
                pltpu.VMEM((4, rows, COLS), F32),
                pltpu.VMEM((4, 2, 2, block, LANES), F32),
                pltpu.VMEM((chunks, rows, COLS), BF16),
                pltpu.VMEM((chunks, rows, COLS), BF16),
                halves((2,), block), halves((2,), block),
                halves((), block), halves((), block),
                halves((2,), piece), halves((2,), piece),
                halves((), piece), halves((), piece),
                pltpu.VMEM((2, chunks, COLS // LANES, rows, LANES), BF16),
                dma((2, splits)), dma((2, 2)), dma(()), dma((10,)),
                dma((chunks,)), *[dma((chunks, 2, 2))] * 8, dma((chunks,)),
            ],
            compiler_params=pltpu.CompilerParams(
                collective_id=0, has_side_effects=True, vmem_limit_bytes=63 * 2**20),
        )(a, g)

    return jax.shard_map(
        step, mesh=mesh, in_specs=(P(("rep", "dp")), P(("rep", "dp"))), out_specs=P("rep"), check_vma=False)
```

time: 178 us -> 129 us (0.72)
  blocking collectives: 133 us -> 0 us
  Pallas kernels: 0 us -> 121 us
  matrix products: 45.1 us -> 0 us
  local copies, waits for them, and re-layouts: 0 us -> 7.89 us
    dot_general x1 -> x0, blocking collectives: 133 us -> none  [step(): jnp.einsum('rsntd,rsntf->rndf', a, g, preferred_element_type=jnp.float32)]
    pallas_call x0 -> x1, Pallas kernels: none -> 121 us  [step(): pl.pallas_call(functools.partial(kernel, side), out_shape=jax.ShapeDtypeS...]
    dot_general x1 -> x0, matrix products: 45.1 us -> none  [step(): jnp.einsum('rsntd,rsntf->rndf', a, g, preferred_element_type=jnp.float32)]
    unnamed x0 -> x1, local copies, waits for them, and re-layouts: none -> 7.89 us
where the time goes in v1:
time: 129 us
  Pallas kernels  121 us (94%)
  local copies, waits for them, and re-layouts  7.89 us (6%)
    pallas_call x1, Pallas kernels, step(): pl.pallas_call(functools.partial(kernel, side), out_shape=jax.ShapeDtypeS...  121 us
    unnamed x1, local copies, waits for them, and re-layouts  7.89 us

profile of v1, /device:TPU:97, one launch (start us, length us, event | category | flops | bytes accessed | tf_op | source)
XLA Modules:
  0.0 129.3 jit_solution(16580690963969272528)
XLA Ops:
  0.0 121.4 %shard_map.28 = bf16[2,512,4096]{2,1,0:T(8,128)(2,1)} custom-call(bf16[1,2,4096,512]{3,2,1,0:T(8,128)(2,1)} %a_ref.1, bf16[1,2,4096,4096]{3,2,1,0:T(8,128)(2,1)} %g_ref.1), custom_call_target="tpu_custom_call" | custom-call | tf_op jit(solution)/shard_map/pallas_call | solution.py:292
  121.4 7.9 %copy.4 = bf16[2,512,4096]{2,1,0:T(8,128)(2,1)} copy(bf16[2,512,4096]{2,1,0:T(8,128)(2,1)} %shard_map.28) | data formatting | bytes 16777216

commit v2 on v0

v2 whole, which is shorter than its diff:
```python
import functools
import math

import jax
import jax.numpy as jnp
from jax import lax
from jax.experimental import pallas as pl
from jax.experimental.pallas import tpu as pltpu
from jax.sharding import PartitionSpec as P

MESH = pl.DeviceIdType.MESH
F32, BF16 = jnp.float32, jnp.bfloat16
COLS = 512
VMEM_LIMIT = 54
LAGS = (1, 3, 5, 7, 9, 10)


def sum_kernel(side, a_ref, g_ref, ag, av, gv, acc, mid, es, er, s1, r1, s2, r2,
               a_sem, g_sem, send_sem, e_r, r1_r, r2_r, g2_r, g1_r, z_r):
    chunks, rows = es.shape[0], es.shape[1]
    splits = av.shape[1]
    block, piece = rows // side, rows // side // side
    ring, ring_mid = acc.shape[0], mid.shape[0]

    me = lax.axis_index("dp")
    core = lax.rem(me, 2)
    y = lax.rem(lax.div(me, 2), side)
    x = lax.div(me, 2 * side)

    def device(x, y, core):
        return (x * side + y) * 2 + core

    def up(p, by):
        return lax.rem(p + by, side)

    steps = tuple(range(1, side))
    far_first = sorted(steps, key=lambda k: -min(k, side - k))
    peer = device(x, y, 1 - core)
    on_x = [device(up(x, k), y, core) for k in steps]
    on_y = [device(x, up(y, k), core) for k in steps]

    def axes(s):
        odd = lax.rem(s, 2)

        def pick(u, v):
            return jnp.where(odd == 0, u, v)

        return (pick(x, y), pick(y, x), [pick(u, v) for u, v in zip(on_x, on_y)],
                [pick(v, u) for u, v in zip(on_x, on_y)])

    def a_copy(m, h):
        matrix = 1 - core if m == 0 else core
        return pltpu.make_async_copy(a_ref.at[0, matrix, :, pl.ds(h * rows, rows)], av.at[m, h], a_sem.at[m, h])

    def g_copy(m, j, slot):
        matrix = 1 - core if m == 0 else core
        columns = pl.ds(pl.multiple_of(j * COLS, COLS), COLS)
        return pltpu.make_async_copy(g_ref.at[0, matrix, :, columns], gv.at[m, slot], g_sem.at[m, slot])

    for m in range(2):
        a_copy(m, 0).start()
        g_copy(m, 0, 0).start()
    for m in range(2):
        for h in range(1, splits):
            a_copy(m, h).start()

    barrier = pltpu.get_barrier_semaphore()
    partners = (peer, *on_x, *on_y)
    for partner in partners:
        pl.semaphore_signal(barrier, inc=1, device_id={"dp": partner}, device_id_type=MESH)

    def remote(src, dst, stage, recv, to):
        return pltpu.make_async_remote_copy(
            src_ref=src, dst_ref=dst, send_sem=send_sem.at[stage], recv_sem=recv, device_id={"dp": to},
            device_id_type=MESH)

    def at(p, size):
        return pl.ds(pl.multiple_of(p * size, size), size)

    def e_copy(s):
        return remote(es.at[s], er.at[s], 0, e_r.at[s], peer)

    def r1_copy(s, k, to):
        return remote(s1.at[s, k - 1], r1.at[s, k - 1], 1, r1_r.at[s, k - 1], to)

    def r2_copy(s, k, to):
        return remote(s2.at[s, k - 1], r2.at[s, k - 1], 2, r2_r.at[s, k - 1], to)

    def g2_copy(s, k, to, p, q):
        view = ag.at[0, s, at(p * side + q, piece)]
        return remote(view, view, 3, g2_r.at[s, k - 1], to)

    def g1_copy(s, k, to, p):
        view = ag.at[0, s, at(p, block)]
        return remote(view, view, 4, g1_r.at[s, k - 1], to)

    def z_copy(s):
        return remote(ag.at[0, s], ag.at[1, s], 5, z_r.at[s], peer)

    def do_e(s):
        c = lax.rem(s, ring)
        p, _, first, _ = axes(s)
        e_copy(s).wait_recv()
        acc[c] += er[s].astype(F32)
        for k in far_first:
            s1[s, k - 1] = acc[c, at(up(p, k), block)].astype(BF16)
            r1_copy(s, k, first[k - 1]).start()

    def do_r2(s):
        c, d = lax.rem(s, ring), lax.rem(s, ring_mid)
        p, q, first, second = axes(s)
        for k in steps:
            r1_copy(s, k, first[k - 1]).wait_recv()
        total = acc[c, at(p, block)]
        for k in steps:
            total += r1[s, k - 1].astype(F32)
        mid[d] = total
        for k in far_first:
            s2[s, k - 1] = mid[d, at(up(q, k), piece)].astype(BF16)
            r2_copy(s, k, second[k - 1]).start()

    def do_g2(s):
        d = lax.rem(s, ring_mid)
        p, q, _, second = axes(s)
        for k in steps:
            r2_copy(s, k, second[k - 1]).wait_recv()
        total = mid[d, at(q, piece)]
        for k in steps:
            total += r2[s, k - 1].astype(F32)
        ag[0, s, at(p * side + q, piece)] = total.astype(BF16)
        for k in far_first:
            g2_copy(s, k, second[k - 1], p, q).start()

    def do_g1(s):
        p, q, first, second = axes(s)
        for k in steps:
            g2_copy(s, k, second[k - 1], p, q).wait_recv()
        for k in far_first:
            g1_copy(s, k, first[k - 1], p).start()

    def do_z(s):
        p, _, first, _ = axes(s)
        for k in steps:
            g1_copy(s, k, first[k - 1], p).wait_recv()
        z_copy(s).start()

    def do_end(s):
        z_copy(s).wait_recv()

    later = (do_e, do_r2, do_g2, do_g1, do_z, do_end)

    def term(m, h, slot):
        return lax.dot_general(av[m, h], gv[m, slot], (((0,), (0,)), ((), ())), preferred_element_type=F32)

    def turn(i, carry):
        j, h = lax.div(i, splits), lax.rem(i, splits)
        slot = lax.rem(j, 2)
        computes = i < chunks

        @pl.when(computes)
        def _():
            @pl.when(h == 0)
            def _():
                @pl.when(i + splits < chunks)
                def _():
                    for m in range(2):
                        g_copy(m, j + 1, 1 - slot).start()

                g_copy(0, j, slot).wait()

            @pl.when(j == 0)
            def _():
                a_copy(0, h).wait()

            es[i] = term(0, h, slot).astype(BF16)

            @pl.when(i == 0)
            def _():
                pl.semaphore_wait(barrier, len(partners))

            e_copy(i).start()

        for lag, step in zip(LAGS, later):
            s = i - lag

            @pl.when((s >= 0) & (s < chunks))
            def _():
                step(s)

        @pl.when(computes)
        def _():
            @pl.when(h == 0)
            def _():
                g_copy(1, j, slot).wait()

            @pl.when(j == 0)
            def _():
                a_copy(1, h).wait()

            acc[lax.rem(i, ring)] = term(1, h, slot)

        return carry

    lax.fori_loop(0, chunks + LAGS[-1], turn, 0)

    sent = [es, s1, s2, s2, s1, es]
    for stage, ref in enumerate(sent):
        pltpu.make_async_copy(ref, ref, send_sem.at[stage]).wait()


def out_kernel(splits, v_ref, out_ref, sem):
    _, chunks, rows, columns = v_ref.shape
    core = lax.rem(lax.axis_index("dp"), 2)
    copies = []
    for m in range(2):
        for s in range(chunks):
            j, h = s // splits, s % splits
            copies.append(pltpu.make_async_copy(
                v_ref.at[m, s],
                out_ref.at[core if m == 0 else 1 - core, pl.ds(h * rows, rows), pl.ds(j * columns, columns)],
                sem.at[m, s]))
    for copy in copies:
        copy.start()
    for copy in copies:
        copy.wait()


def solution(mesh):
    side = math.isqrt(mesh.shape["dp"] // 2)

    def step(a, g):
        _, matrices, tokens, d = a.shape
        ff = g.shape[3]
        assert matrices == 2
        splits = 2
        rows = d // splits
        chunks = splits * ff // COLS
        block, piece = rows // side, rows // side // side
        others = side - 1
        ring = LAGS[1] + 1
        ring_mid = LAGS[2] - LAGS[1] + 1
        dma = pltpu.SemaphoreType.DMA
        gathered = pl.pallas_call(
            functools.partial(sum_kernel, side),
            out_shape=pltpu.VMEM((matrices, chunks, rows, COLS), BF16),
            in_specs=[pl.BlockSpec(memory_space=pl.ANY)] * 2,
            out_specs=pl.BlockSpec(memory_space=pltpu.VMEM),
            scratch_shapes=[
                pltpu.VMEM((2, splits, tokens, rows), BF16),
                pltpu.VMEM((2, 2, tokens, COLS), BF16),
                pltpu.VMEM((ring, rows, COLS), F32),
                pltpu.VMEM((ring_mid, block, COLS), F32),
                pltpu.VMEM((chunks, rows, COLS), BF16),
                pltpu.VMEM((chunks, rows, COLS), BF16),
                pltpu.VMEM((chunks, others, block, COLS), BF16),
                pltpu.VMEM((chunks, others, block, COLS), BF16),
                pltpu.VMEM((chunks, others, piece, COLS), BF16),
                pltpu.VMEM((chunks, others, piece, COLS), BF16),
                dma((2, splits)), dma((2, 2)), dma((6,)),
                dma((chunks,)), *[dma((chunks, others))] * 4, dma((chunks,)),
            ],
            compiler_params=pltpu.CompilerParams(
                collective_id=0, has_side_effects=True, vmem_limit_bytes=VMEM_LIMIT * 2**20),
        )(a, g)
        return pl.pallas_call(
            functools.partial(out_kernel, splits),
            out_shape=jax.ShapeDtypeStruct((matrices, d, ff), BF16),
            in_specs=[pl.BlockSpec(memory_space=pltpu.VMEM)],
            out_specs=pl.BlockSpec(memory_space=pl.ANY),
            scratch_shapes=[dma((matrices, chunks))],
            compiler_params=pltpu.CompilerParams(vmem_limit_bytes=2**20),
        )(gathered)

    return jax.shard_map(
        step, mesh=mesh, in_specs=(P(("rep", "dp")), P(("rep", "dp"))), out_specs=P("rep"), check_vma=False)
```

time: 178 us -> 91.1 us (0.51)
  blocking collectives: 133 us -> 0 us
  Pallas kernels: 0 us -> 91.1 us
  matrix products: 45.1 us -> 0 us
    dot_general x1 -> x0, blocking collectives: 133 us -> none  [step(): jnp.einsum('rsntd,rsntf->rndf', a, g, preferred_element_type=jnp.float32)]
    pallas_call x0 -> x2, Pallas kernels: none -> 91.1 us  [the longest x1 87.5 us: step(): pl.pallas_call(functools.partial(sum_kernel, side), out_shape=pltpu.VMEM(...]
    dot_general x1 -> x0, matrix products: 45.1 us -> none  [step(): jnp.einsum('rsntd,rsntf->rndf', a, g, preferred_element_type=jnp.float32)]
where the time goes in v2:
time: 91.1 us
  Pallas kernels  91.1 us (100%)
    pallas_call x1, Pallas kernels, step(): pl.pallas_call(functools.partial(sum_kernel, side), out_shape=pltpu.VMEM(...  87.5 us
    pallas_call x1, Pallas kernels, step(): pl.pallas_call(functools.partial(out_kernel, splits), out_shape=jax.Shape...  3.55 us

profile of v2, /device:TPU:97, one launch (start us, length us, event | category | flops | bytes accessed | tf_op | source)
XLA Modules:
  0.0 91.1 jit_solution(16201994803112729486)
XLA Ops:
  0.0 87.5 %shard_map.28.v_ref = bf16[2,16,256,512]{3,2,1,0:T(8,128)(2,1)S(1)} custom-call(bf16[1,2,4096,512]{3,2,1,0:T(8,128)(2,1)} %a_ref.1, bf16[1,2,4096,4096]{3,2,1,0:T(8,128)(2,1)} %g_ref.1), custom_call_target="tpu_custom_call" | custom-call | tf_op jit(solution)/shard_map/pallas_call | solution.py:243
  87.5 3.5 %shard_map.29 = bf16[2,512,4096]{2,1,0:T(8,128)(2,1)} custom-call(bf16[2,16,256,512]{3,2,1,0:T(8,128)(2,1)S(1)} %shard_map.28.v_ref), custom_call_target="tpu_custom_call" | custom-call | tf_op jit(solution)/shard_map/pallas_call | solution.py:265

commit v3 on v2

v3 whole, which is shorter than its diff:
```python
import functools
import math

import jax
import jax.numpy as jnp
from jax import lax
from jax.experimental import pallas as pl
from jax.experimental.pallas import tpu as pltpu
from jax.sharding import PartitionSpec as P

MESH = pl.DeviceIdType.MESH
F32, BF16 = jnp.float32, jnp.bfloat16
COLS = 512
HALF = COLS // 2
VMEM_LIMIT = 54
LAST = 2
RING = (("r2", 5, 4.8), ("g2", 8, 3.6), ("g1", 11, 3.6), ("g1_next", 15, 4.0), ("z", 22, 3.5), ("end", 24, 1.3))
LONG = (("r2", 4, 4.8), ("g2", 7, 3.6), ("g1", 10, 3.6), ("z", 14, 4.8), ("end", 16, 1.3))
TURN = 3.15


def last_steps(chunks):
    ready = []
    for s in range(chunks):
        kind = kind_of(s, chunks)
        before = (s + 1 - chunks) * TURN
        for n, (name, lag, hop) in enumerate(kind):
            if s + (lag + 1) // 2 < chunks:
                before = (s + 1 - chunks) * TURN + lag * TURN / 2
            else:
                ready.append((before + hop, n, s, name))
                before = max(before + hop, 0.0)
    return [(s, name) for _, _, s, name in sorted(ready)]


def kind_of(s, chunks):
    return RING if s < chunks - LAST else LONG


def sum_kernel(side, a_ref, g_ref, ag, av, gv, acc, mid, es, er, s1, r1, s2, r2,
               a_sem, g_sem, send_sem, e_r, r1_r, r2_r, g2_r, g1_r, m1_r, z_r):
    chunks, rows = es.shape[0], es.shape[1]
    splits = av.shape[1]
    block, piece = rows // side, rows // side // side
    ring, ring_mid = acc.shape[0], mid.shape[0]

    me = lax.axis_index("dp")
    core = lax.rem(me, 2)
    y = lax.rem(lax.div(me, 2), side)
    x = lax.div(me, 2 * side)

    def device(x, y, core):
        return (x * side + y) * 2 + core

    def up(p, by):
        return lax.rem(p + by, side)

    steps = tuple(range(1, side))
    far_first = sorted(steps, key=lambda k: -min(k, side - k))
    peer = device(x, y, 1 - core)
    on_x = [device(up(x, k), y, core) for k in steps]
    on_y = [device(x, up(y, k), core) for k in steps]

    def rem(s, n):
        return s % n if isinstance(s, int) else lax.rem(s, n)

    def axes(s):
        odd = rem(s, 2)

        def pick(u, v):
            return (v if odd else u) if isinstance(s, int) else jnp.where(odd == 0, u, v)

        return (pick(x, y), pick(y, x), [pick(u, v) for u, v in zip(on_x, on_y)],
                [pick(v, u) for u, v in zip(on_x, on_y)])

    def a_copy(m, h):
        matrix = 1 - core if m == 0 else core
        return pltpu.make_async_copy(a_ref.at[0, matrix, :, pl.ds(h * rows, rows)], av.at[m, h], a_sem.at[m, h])

    def g_copy(m, j, slot):
        matrix = 1 - core if m == 0 else core
        columns = pl.ds(pl.multiple_of(j * COLS, COLS), COLS)
        return pltpu.make_async_copy(g_ref.at[0, matrix, :, columns], gv.at[m, slot], g_sem.at[m, slot])

    a_copy(0, 0).start()
    g_copy(0, 0, 0).start()

    barrier = pltpu.get_barrier_semaphore()
    partners = (peer, *on_x, *on_y)
    for partner in partners:
        pl.semaphore_signal(barrier, inc=1, device_id={"dp": partner}, device_id_type=MESH)

    def remote(src, dst, stage, recv, to):
        return pltpu.make_async_remote_copy(
            src_ref=src, dst_ref=dst, send_sem=send_sem.at[stage], recv_sem=recv, device_id={"dp": to},
            device_id_type=MESH)

    def at(p, size):
        return pl.ds(pl.multiple_of(p * size, size), size)

    def e_copy(s):
        return remote(es.at[s], er.at[s], 0, e_r.at[s], peer)

    def z_copy(s):
        return remote(ag.at[0, s], ag.at[1, s], 5, z_r.at[s], peer)

    def r1_copy(s, k, to):
        part = pl.ds(2 * (k - 1), 2)
        return remote(s1.at[s, part], r1.at[s, part], 1, r1_r.at[s], to)

    def r2_copy(s, k, to):
        return remote(s2.at[s, k - 1], r2.at[s, k - 1], 2, r2_r.at[s], to)

    def g2_copy(s, k, to, p, q):
        view = ag.at[0, s, at(p * side + q, piece)]
        return remote(view, view, 3, g2_r.at[s], to)

    def g1_copy(s, to, p):
        view = ag.at[0, s, at(p, block)]
        return remote(view, view, 4, g1_r.at[s], to)

    def g1_next(s, way, to, p):
        view = ag.at[0, s, at(p, block), pl.ds(way * HALF, HALF)]
        return remote(view, view, 4, m1_r.at[s], to)

    def landed(ref, sem):
        pltpu.make_async_copy(ref, ref, sem).wait()

    def half(h):
        return slice(h * HALF, (h + 1) * HALF)

    def ends(first):
        return first[0], first[-1]

    def start_r1(s):
        c = rem(s, ring)
        p, _, first, _ = axes(s)
        for k in far_first:
            for h in range(2):
                s1[s, 2 * (k - 1) + h] = acc[c, at(up(p, k), block), half(h)].astype(BF16)
            r1_copy(s, k, first[k - 1]).start()

    def do_r2(s, straight):
        c, d = rem(s, ring), rem(s, ring_mid)
        p, q, _, second = axes(s)
        landed(r1.at[s], r1_r.at[s])
        for h in range(2):
            total = acc[c, at(p, block), half(h)]
            for k in steps:
                total += r1[s, 2 * (k - 1) + h].astype(F32)
            mid[d, :, half(h)] = total
        for k in far_first:
            s2[s, k - 1] = mid[d, at(up(q, k), piece)].astype(BF16)
            r2_copy(s, k, second[k - 1]).start()

    def do_g2(s, straight):
        d = rem(s, ring_mid)
        p, q, _, second = axes(s)
        landed(r2.at[s], r2_r.at[s])
        total = mid[d, at(q, piece)]
        for k in steps:
            total += r2[s, k - 1].astype(F32)
        ag[0, s, at(p * side + q, piece)] = total.astype(BF16)
        for k in far_first:
            g2_copy(s, k, second[k - 1], p, q).start()

    def do_g1(s, straight):
        p, q, first, second = axes(s)
        landed(r2.at[s], g2_r.at[s])
        if straight:
            for k in far_first:
                g1_copy(s, first[k - 1], p).start()
        else:
            for way, to in enumerate(ends(first)):
                g1_copy(s, to, p).start()

    def do_g1_next(s, straight):
        p, _, first, _ = axes(s)
        landed(r1.at[s, 0:4], g1_r.at[s])
        for way, to in enumerate(ends(first)):
            g1_next(s, way, to, up(p, side - 1 if way == 0 else 1)).start()

    def do_z(s, straight):
        p, _, first, _ = axes(s)
        if straight:
            landed(r1.at[s], g1_r.at[s])
        else:
            landed(r1.at[s, 4:6], m1_r.at[s])
        z_copy(s).start()

    def do_end(s, straight):
        z_copy(s).wait_recv()

    steps_of = dict(r2=do_r2, g2=do_g2, g1=do_g1, g1_next=do_g1_next, z=do_z, end=do_end)
    kinds = ((RING, 0, chunks - LAST), (LONG, chunks - LAST, chunks))

    def term(m, h, slot):
        return lax.dot_general(av[m, h], gv[m, slot], (((0,), (0,)), ((), ())), preferred_element_type=F32)

    def due(i, odd):
        for kind, low, high in kinds:
            for name, lag, _ in kind:
                turns = (lag + 1) // 2
                if lag % 2 == odd and low < high and low + turns < chunks:

                    @pl.when((i - turns >= low) & (i - turns < high))
                    def _():
                        steps_of[name](i - turns, kind is LONG)

    def turn(i, carry):
        n = i + 1
        j, h = lax.div(n, splits), lax.rem(n, splits)
        slot = lax.rem(j, 2)

        @pl.when(n < chunks)
        def _():
            @pl.when(h == 0)
            def _():
                @pl.when((n > 0) & (n + splits < chunks))
                def _():
                    g_copy(0, j + 1, 1 - slot).start()

                g_copy(0, j, slot).wait()

            @pl.when(j == 0)
            def _():
                a_copy(0, h).wait()

            @pl.when(n == 0)
            def _():
                for h in range(1, splits):
                    a_copy(0, h).start()
                a_copy(1, 0).start()
                g_copy(1, 0, 0).start()
                for h in range(1, splits):
                    a_copy(1, h).start()
                g_copy(0, 1, 1).start()

            es[n] = term(0, h, slot).astype(BF16)

            @pl.when(n == 0)
            def _():
                pl.semaphore_wait(barrier, len(partners))

            e_copy(n).start()

        due(i, 1)

        @pl.when(i >= 0)
        def _():
            j, h = lax.div(i, splits), lax.rem(i, splits)
            slot = lax.rem(j, 2)

            @pl.when(h == 0)
            def _():
                @pl.when(i + splits < chunks)
                def _():
                    g_copy(1, j + 1, 1 - slot).start()

                g_copy(1, j, slot).wait()

            @pl.when(j == 0)
            def _():
                a_copy(1, h).wait()

            e_copy(i).wait_recv()
            acc[lax.rem(i, ring)] = term(1, h, slot) + er[i].astype(F32)
            start_r1(i)

        due(i, 0)
        return carry

    lax.fori_loop(-1, chunks, turn, 0)
    for s, name in last_steps(chunks):
        steps_of[name](s, kind_of(s, chunks) is LONG)

    sent = [es, s1, s2, s2, s1, es]
    for stage, ref in enumerate(sent):
        pltpu.make_async_copy(ref, ref, send_sem.at[stage]).wait()


def out_kernel(splits, v_ref, out_ref, sem):
    _, chunks, rows, columns = v_ref.shape
    core = lax.rem(lax.axis_index("dp"), 2)
    copies = []
    for m in range(2):
        for s in range(chunks):
            j, h = s // splits, s % splits
            copies.append(pltpu.make_async_copy(
                v_ref.at[m, s],
                out_ref.at[core if m == 0 else 1 - core, pl.ds(h * rows, rows), pl.ds(j * columns, columns)],
                sem.at[m, s]))
    for copy in copies:
        copy.start()
    for copy in copies:
        copy.wait()


def solution(mesh):
    side = math.isqrt(mesh.shape["dp"] // 2)

    def step(a, g):
        _, matrices, tokens, d = a.shape
        ff = g.shape[3]
        assert matrices == 2 and side == 4
        splits = 2
        rows = d // splits
        chunks = splits * ff // COLS
        block, piece = rows // side, rows // side // side
        others = side - 1
        ring = 8
        ring_mid = 8
        dma = pltpu.SemaphoreType.DMA
        gathered = pl.pallas_call(
            functools.partial(sum_kernel, side),
            out_shape=pltpu.VMEM((matrices, chunks, rows, COLS), BF16),
            in_specs=[pl.BlockSpec(memory_space=pl.ANY)] * 2,
            out_specs=pl.BlockSpec(memory_space=pltpu.VMEM),
            scratch_shapes=[
                pltpu.VMEM((2, splits, tokens, rows), BF16),
                pltpu.VMEM((2, 2, tokens, COLS), BF16),
                pltpu.VMEM((ring, rows, COLS), F32),
                pltpu.VMEM((ring_mid, block, COLS), F32),
                pltpu.VMEM((chunks, rows, COLS), BF16),
                pltpu.VMEM((chunks, rows, COLS), BF16),
                pltpu.VMEM((chunks, 6, block, HALF), BF16),
                pltpu.VMEM((chunks, 6, block, HALF), BF16),
                pltpu.VMEM((chunks, others, piece, COLS), BF16),
                pltpu.VMEM((chunks, others, piece, COLS), BF16),
                dma((2, splits)), dma((2, 2)), dma((6,)),
                *[dma((chunks,))] * 7,
            ],
            compiler_params=pltpu.CompilerParams(
                collective_id=0, has_side_effects=True, vmem_limit_bytes=VMEM_LIMIT * 2**20),
        )(a, g)
        return pl.pallas_call(
            functools.partial(out_kernel, splits),
            out_shape=jax.ShapeDtypeStruct((matrices, d, ff), BF16),
            in_specs=[pl.BlockSpec(memory_space=pltpu.VMEM)],
            out_specs=pl.BlockSpec(memory_space=pl.ANY),
            scratch_shapes=[dma((matrices, chunks))],
            compiler_params=pltpu.CompilerParams(vmem_limit_bytes=2**20),
        )(gathered)

    return jax.shard_map(
        step, mesh=mesh, in_specs=(P(("rep", "dp")), P(("rep", "dp"))), out_specs=P("rep"), check_vma=False)
```

time: 91.1 us -> 84.7 us (0.930)
  Pallas kernels: 91.1 us -> 84.6 us
    pallas_call x1, Pallas kernels: 87.5 us -> 81 us  [step(): pl.pallas_call(functools.partial(sum_kernel, side), out_shape=pltpu.VMEM(...]
where the time goes in v3:
time: 84.7 us; the launch traced here: 84.6 us
  Pallas kernels  84.6 us (100%)
    pallas_call x1, Pallas kernels, step(): pl.pallas_call(functools.partial(sum_kernel, side), out_shape=pltpu.VMEM(...  81 us
    pallas_call x1, Pallas kernels, step(): pl.pallas_call(functools.partial(out_kernel, splits), out_shape=jax.Shape...  3.55 us

profile of v3, /device:TPU:97, one launch (start us, length us, event | category | flops | bytes accessed | tf_op | source)
XLA Modules:
  0.0 84.6 jit_solution(6245115534457338957)
XLA Ops:
  0.0 81.0 %shard_map.28.v_ref = bf16[2,16,256,512]{3,2,1,0:T(8,128)(2,1)S(1)} custom-call(bf16[1,2,4096,512]{3,2,1,0:T(8,128)(2,1)} %a_ref.1, bf16[1,2,4096,4096]{3,2,1,0:T(8,128)(2,1)} %g_ref.1), custom_call_target="tpu_custom_call" | custom-call | tf_op jit(solution)/shard_map/pallas_call | solution.py:314
  81.0 3.5 %shard_map.29 = bf16[2,512,4096]{2,1,0:T(8,128)(2,1)} custom-call(bf16[2,16,256,512]{3,2,1,0:T(8,128)(2,1)S(1)} %shard_map.28.v_ref), custom_call_target="tpu_custom_call" | custom-call | tf_op jit(solution)/shard_map/pallas_call | solution.py:336
